TPU v7x, 256 devices: a whole 4x4x8 slice. The times are simulated.
256 devices in a mesh: space: 32 (over y, z_lo, core), scene: 8 (over x, z_hi).
Axes of the slice: x: 4, y: 4, z: 8 (z_hi: 2, z_lo: 4; z = z_hi * 4 + z_lo), core: 2. Of those that a mesh axis runs over, the one named last changes fastest.
Arguments:
- grad_out: bfloat16 [8, 64, 128, 256], P('scene', 'space'), may hold values from -6 to 6
- pre_second: bfloat16 [8, 64, 128, 256], P('scene', 'space'), may hold values from -6 to 6
- pre_first: bfloat16 [8, 64, 128, 256], P('scene', 'space'), may hold values from -6 to 6
- camera_bev: bfloat16 [8, 64, 128, 80], P('scene', 'space'), may hold values from -6 to 6
- lidar_bev: bfloat16 [8, 64, 128, 256], P('scene', 'space'), may hold values from -6 to 6
- weight_a: bfloat16 [256, 3024], replicated, may hold values from -0.109375 to 0.109375
- weight_b: bfloat16 [256, 2304], replicated, may hold values from -0.125 to 0.125
- depth_weights: bfloat16 [8, 118, 4096], P('scene', None, 'space'), may hold values from 0 to 1
- context: bfloat16 [8, 80, 4096], P('scene', None, 'space'), may hold values from -6 to 6
- block_list: int32 [32, 32, 1], P(None, 'space'), may hold values from -1 to 1, as said below
- point_slot: int32 [118, 4096], P(None, 'space'), may hold values from 0 to 4095, as said below
Outputs:
- weight_grad_a: float32 [256, 3024], P('space')
- weight_grad_b: float32 [256, 2304], P('space')
- grad_lidar: bfloat16 [8, 64, 128, 256], P('scene', 'space')
- grad_context: float32 [8, 80, 4096], P('scene', None, 'space')
- grad_depth: float32 [8, 118, 4096], P('scene', None, 'space')
Inputs may be any that keep to these rules, and one draw needn't show every extreme that they name: block_list[d, s, k] is a block of 128 cells of device s's rows owed to frustum owner d, distinct within (d, s), or -1 for an empty slot; live slots come first; every owner has a live slot from itself; in every draw some owner has all 1 slots live from every device. point_slot[d, p] = (s + k) * 128 + q names cell q of the block in a live slot k from device s, for the owner of pixel p.
All inputs are finite; a program needn't handle non-finite values.
Results may differ from a plain program's by a relative error of at most 0.005.
Values may be sent and summed in bfloat16 or wider, within the bound.
No kernel may reach another device: no remote copies, remote signals or barrier semaphores. Data moves between devices by JAX's collectives and lax.ppermute only.
A program may use at most 64 MiB of HBM per device.

v0:
```python
import math

import jax
import jax.numpy as jnp
from jax import lax
from jax.sharding import PartitionSpec as P

BLOCK = 128


def split_up(x, dim, devices):
    before, after = (x.shape[:dim], x.shape[dim + 1 :])
    return jnp.moveaxis(x.reshape(*before, devices, -1, *after), dim, 0)


def sent_and_summed(x, axis, dim):
    devices = lax.axis_size(axis)
    blocks = lax.all_to_all(split_up(x, dim, devices), axis, 0, 0, tiled=True)
    return jnp.sum(blocks, axis=0)


def sent_to_all(x, axis):
    copies = jnp.broadcast_to(x, (lax.axis_size(axis), *x.shape))
    return lax.all_to_all(copies, axis, split_axis=0, concat_axis=0, tiled=True)


def taken_together(x, axis):
    everything = sent_to_all(x, axis)
    return jnp.sum(everything, axis=0)


def extended_2(x, sides, width):
    for axis, dim in sides:
        devices, length = (lax.axis_size(axis), x.shape[dim])
        up = [(i, (i + 1) % devices) for i in range(devices - 1)]
        down = [(j, i) for i, j in up]
        last = lax.slice_in_dim(x, length - width, length, axis=dim)
        leading = lax.slice_in_dim(x, 0, width, axis=dim)
        before = lax.ppermute(last, axis, up)
        after = lax.ppermute(leading, axis, down)
        x = jnp.concatenate([before, x, after], axis=dim)
    return x


def taps_of(padded):
    out_rows = padded.shape[0] - 2
    out_cols = padded.shape[1] - 2
    pieces = [
        padded[row_tap : row_tap + out_rows, col_tap : col_tap + out_cols]
        for row_tap in range(3)
        for col_tap in range(3)
    ]
    return jnp.concatenate(pieces, axis=-1).reshape(out_rows * out_cols, -1)


def pad_columns(field):
    return jnp.pad(field, ((0, 0), (1, 1), (0, 0)))


def flipped(weight, fan_channels):
    outputs = weight.shape[0]
    shaped = weight.reshape(outputs, 3, 3, fan_channels)[:, ::-1, ::-1, :]
    return jnp.transpose(shaped, (1, 2, 0, 3)).reshape(9 * outputs, fan_channels)


def back_conv(extended, weight, fan_channels):
    out_rows = extended.shape[0] - 2
    product = jnp.dot(
        taps_of(pad_columns(extended)),
        flipped(weight, fan_channels),
        preferred_element_type=jnp.float32,
    )
    return product.reshape(out_rows, extended.shape[1], fan_channels)


def reduce_weights(grad_flat, patches):
    own_share = sent_and_summed(
        jnp.dot(grad_flat.T, patches, preferred_element_type=jnp.float32), "space", 0
    )
    result = taken_together(own_share, "scene")
    return result


def shards(
    grad_out,
    pre_second,
    pre_first,
    camera_bev,
    lidar_bev,
    weight_a,
    weight_b,
    depth_weights,
    context,
    block_list,
    point_slot,
):
    grad_field = grad_out[0]
    second_pre = pre_second[0]
    first_pre = pre_first[0]
    camera = camera_bev[0]
    lidar_field = lidar_bev[0]
    slab_rows, columns, channels = grad_field.shape
    camera_channels = camera.shape[-1]
    zero_value = jnp.zeros((), jnp.bfloat16)
    float_zero = jnp.zeros((), jnp.float32)
    stacked = jnp.concatenate([first_pre, camera, lidar_field], axis=-1)
    stacked_ext = extended_2(stacked, (("space", 0),), 1)
    first_ext = stacked_ext[..., :channels]
    hidden_ext = jnp.maximum(first_ext, zero_value)
    inputs_ext = stacked_ext[..., channels:]
    paired = jnp.concatenate([grad_field, second_pre], axis=-1)
    paired_ext = extended_2(paired, (("space", 0),), 2)
    grad_b_wide = jnp.where(paired_ext[..., channels:] > 0, paired_ext[..., :channels], zero_value)
    grad_b = grad_b_wide[2:-2]
    back_hidden = back_conv(grad_b_wide, weight_b, channels)
    grad_a_ext = jnp.where(first_ext > 0, back_hidden, float_zero).astype(jnp.bfloat16)
    grad_a = grad_a_ext[1:-1]
    wgrad_b = reduce_weights(grad_b.reshape(-1, channels), taps_of(pad_columns(hidden_ext)))
    wgrad_a = reduce_weights(grad_a.reshape(-1, channels), taps_of(pad_columns(inputs_ext)))
    back_inputs = back_conv(grad_a_ext, weight_a, inputs_ext.shape[-1])
    back_camera = back_inputs[..., :camera_channels].astype(jnp.bfloat16)
    back_lidar = back_inputs[..., camera_channels:].astype(jnp.bfloat16)
    cell_count = slab_rows * columns * lax.axis_size("space") * lax.axis_size("scene")
    norm_factor = 1.0 / math.sqrt(cell_count)
    listing = block_list[:, 0, :]
    blocks = back_camera.reshape(-1, BLOCK * camera_channels)
    picked = jnp.take(blocks, jnp.maximum(listing, 0), axis=0)
    outgoing = jnp.where((listing >= 0)[..., None], picked, zero_value)
    incoming = lax.all_to_all(outgoing, "space", split_axis=0, concat_axis=0, tiled=True)
    received_rows = incoming.reshape(-1, camera_channels)
    gathered = jnp.take(received_rows, point_slot, axis=0)
    grad_context = jnp.einsum(
        "dp,dpc->cp", depth_weights[0], gathered, preferred_element_type=jnp.float32
    )
    grad_depth = jnp.einsum("cp,dpc->dp", context[0], gathered, preferred_element_type=jnp.float32)
    return (
        wgrad_a * norm_factor,
        wgrad_b * norm_factor,
        back_lidar[None],
        grad_context[None],
        grad_depth[None],
    )


def solution(mesh):
    placed = (
        P("scene", "space", None, None),
        P("scene", "space", None, None),
        P("scene", "space", None, None),
        P("scene", "space", None, None),
        P("scene", "space", None, None),
        P(),
        P(),
        P("scene", None, "space"),
        P("scene", None, "space"),
        P(None, "space", None),
        P(None, "space"),
    )
    return jax.shard_map(
        shards,
        mesh=mesh,
        in_specs=placed,
        out_specs=(
            P("space", None),
            P("space", None),
            P("scene", "space", None, None),
            P("scene", None, "space"),
            P("scene", None, "space"),
        ),
        check_vma=False,
    )
```

profile of v0, /device:TPU:2, one launch (start us, length us, event | category | flops | bytes accessed | tf_op | source)
XLA Modules:
  0.0 295.7 jit_solution(17525783439096529744)
XLA Ops:
  1.7 2.5 collective-permute-start.2
  8.2 4.0 %collective-permute-start = (bf16[1,128,592]{2,1,0:T(8,128)(2,1)}, bf16[1,128,592]{2,1,0:T(8,128)(2,1)S(1)}, u32[]{:S(2)}, u32[]{:S(2)}) collective-permute-start(bf16[1,128,592]{2,1,0:T(8,128)(2,1)} %get-tuple-element.40), channel_id=1, source_target_pairs={{0,8},{8,16},{16,24},{24,32},{32,40},{40,48},{48,56},{56,64},{64,7... | collective-permute-start | bytes 454664 | tf_op jit(solution)/shard_map/ppermute | solution.py:39
  16.4 2.2 copy.104
  32.6 12.3 %all-to-all-start.4 = ((bf16[32,2,5120]{2,1,0:T(2,128)(2,1)}), bf16[32,2,5120]{2,1,0:T(2,128)(2,1)S(1)}, u32[]{:S(2)}, u32[]{:S(2)}) async-start(bf16[32,2,5120]{2,1,0:T(2,128)(2,1)} %reshape.189), calls=%async_computation.4 | async-start | bytes 1310720 | tf_op jit(solution)/shard_map/all_to_all | solution.py:129
  50.0 3.2 %fusion.21 = f32[32,8,2304]{2,1,0:T(8,128)} fusion(bf16[256,2304,1]{1,0,2:T(8,128)(2,1)} %bitcast.96, bf16[256,256]{1,0:T(8,128)(2,1)S(1)} %copy.103), kind=kOutput, calls=%fused_computation.73 | convolution fusion | flops 301989888 | bytes 3670016 | tf_op jit(solution)/shard_map/dot_general | solution.py:78
  53.2 11.2 %all-to-all-done.4 = bf16[32,2,5120]{2,1,0:T(2,128)(2,1)S(1)} async-done(((bf16[32,2,5120]{2,1,0:T(2,128)(2,1)}), bf16[32,2,5120]{2,1,0:T(2,128)(2,1)S(1)}, u32[]{:S(2)}, u32[]{:S(2)}) %all-to-all-start.4) | async-done | bytes 655392 | tf_op jit(solution)/shard_map/all_to_all | solution.py:129
  65.2 4.1 %all-to-all-start.2 = ((f32[32,8,2304]{2,1,0:T(8,128)}), f32[32,8,2304]{2,1,0:T(8,128)S(1)}, u32[]{:S(2)}, u32[]{:S(2)}) async-start(f32[32,8,2304]{2,1,0:T(8,128)} %fusion.21), calls=%async_computation.2 | async-start | bytes 4718592 | tf_op jit(solution)/shard_map/all_to_all | solution.py:18
  73.5 1.8 pad_maximum_fusion.4
  77.0 1.8 copy.97
  91.5 3.6 %fusion = f32[32,8,3024]{2,1,0:T(8,128)} fusion(bf16[256,3024]{0,1:T(8,128)(2,1)} %constant_dynamic-update-slice_fusion, bf16[256,256]{1,0:T(8,128)(2,1)S(1)} %copy.92), kind=kOutput, calls=%fused_computation.5 | convolution fusion | flops 396361728 | bytes 4775936 | tf_op jit(solution)/shard_map/dot_general | solution.py:78
  95.2 30.0 %all-to-all-done.2 = f32[32,8,2304]{2,1,0:T(8,128)S(1)} async-done(((f32[32,8,2304]{2,1,0:T(8,128)}), f32[32,8,2304]{2,1,0:T(8,128)S(1)}, u32[]{:S(2)}, u32[]{:S(2)}) %all-to-all-start.2) | async-done | bytes 2359328 | tf_op jit(solution)/shard_map/all_to_all | solution.py:18
  126.7 4.1 %all-to-all-start = ((f32[32,8,3024]{2,1,0:T(8,128)}), f32[32,8,3024]{2,1,0:T(8,128)S(1)}, u32[]{:S(2)}, u32[]{:S(2)}) async-start(f32[32,8,3024]{2,1,0:T(8,128)} %fusion), calls=%async_computation | async-start | bytes 6291456 | tf_op jit(solution)/shard_map/all_to_all | solution.py:18
  131.4 1.8 reduce_sum.38
  133.2 70.4 %all-to-all-done = f32[32,8,3024]{2,1,0:T(8,128)S(1)} async-done(((f32[32,8,3024]{2,1,0:T(8,128)}), f32[32,8,3024]{2,1,0:T(8,128)S(1)}, u32[]{:S(2)}, u32[]{:S(2)}) %all-to-all-start) | async-done | bytes 3096608 | tf_op jit(solution)/shard_map/all_to_all | solution.py:18
  204.5 11.4 %all-to-all-start.3 = ((f32[8,8,2304]{2,1,0:T(8,128)}), f32[8,8,2304]{2,1,0:T(8,128)}, u32[]{:S(2)}, u32[]{:S(2)}) async-start(f32[8,8,2304]{2,1,0:T(8,128)} %broadcast_in_dim.62), calls=%async_computation.3 | async-start | bytes 1179648 | tf_op jit(solution)/shard_map/all_to_all | solution.py:24
  219.8 5.0 %reshape.190 = bf16[32,1,10240]{2,1,0:T(2,128)(2,1)} reshape(bf16[32,2,5120]{2,1,0:T(2,128)(2,1)} %copy-done.3) | data formatting | bytes 1310720
  224.8 5.8 %reduce.2 = bf16[32,10240]{1,0:T(8,128)(2,1)} reduce(bf16[32,1,10240]{2,1,0:T(2,128)(2,1)} %reshape.190, bf16[]{:T(256)} %constant.61), dimensions={1}, to_apply=%all_to_all.19.reduce_sub_computation | reduce | bytes 1310722 | tf_op jit(solution)/shard_map/all_to_all | solution.py:129
  230.6 2.3 reshape.161
  233.0 31.0 %gather_fusion.1 = bf16[15104,80]{1,0:T(8,128)(2,1)} fusion(bf16[4096,80]{1,0:T(8,128)(2,1)S(1)} %reshape.161, s32[15360]{0:T(1024)S(1)} %copy-done.18), kind=kCustom, calls=%fused_computation.1 | custom fusion | bytes 4893696 | tf_op jit(solution)/shard_map/jit(_take)/gather | solution.py:131
  264.0 2.0 reduce_sum.36
  267.0 9.6 %all-to-all-start.1 = ((f32[8,8,3024]{2,1,0:T(8,128)}), f32[8,8,3024]{2,1,0:T(8,128)S(1)}, u32[]{:S(2)}, u32[]{:S(2)}) async-start(f32[8,8,3024]{2,1,0:T(8,128)} %broadcast_in_dim.61), calls=%async_computation.1 | async-start | bytes 1572864 | tf_op jit(solution)/shard_map/all_to_all | solution.py:24
  276.6 7.3 %multiply_reduce_fusion = f32[128,118]{0,1:T(8,128)S(1)} fusion(f32[128,80]{1,0:T(8,128)S(1)} %copy.125, bf16[118,128,80]{2,1,0:T(8,128)(2,1)} %bitcast.86, pred[118,128]{1,0:T(8,128)(4,1)S(1)} %compare_and_fusion), kind=kLoop, calls=%fused_computation.2 | loop fusion | flops 4818176 | bytes 2533120 | tf_op jit(solution)/shard_map/cp,dpc->dp/dot_general | solution.py:135
  284.6 5.3 %multiply_reduce_fusion.1 = f32[128,80]{1,0:T(8,128)S(1)} fusion(f32[128,118]{0,1:T(8,128)S(1)} %copy-done.20, bf16[118,128,80]{2,1,0:T(8,128)(2,1)S(1)} %bitcast.87, pred[118,128]{1,0:T(8,128)(4,1)S(1)} %compare_and_fusion), kind=kLoop, calls=%fused_computation.3 | loop fusion | flops 4823040 | bytes 2533120
  292.4 2.7 all-to-all-done.1
  (150 shorter events, 59.1 us)
Async XLA Ops:
  0.6 12.9 %copy-start.6 = (bf16[256,2304]{1,0:T(8,128)(2,1)S(1)}, bf16[256,2304]{1,0:T(8,128)(2,1)}, u32[]{:S(2)}) copy-start(bf16[256,2304]{1,0:T(8,128)(2,1)} %param.17) | copy-start | bytes 3538948
  1.7 19.1 %collective-permute-start.2 = (bf16[2,128,512]{2,1,0:T(8,128)(2,1)S(1)}, bf16[2,128,512]{2,1,0:T(8,128)(2,1)}, u32[]{:S(2)}, u32[]{:S(2)}) collective-permute-start(bf16[2,128,512]{2,1,0:T(8,128)(2,1)S(1)} %pad_maximum_fusion.3), channel_id=1, source_target_pairs={{0,8},{8,16},{16,24},{24,32},{32,40},{40,48},{48,56},{56,64},{64,7... | collective-permute-start | bytes 786440 | tf_op jit(solution)/shard_map/ppermute | solution.py:39
  4.2 16.6 %collective-permute-start.3 = (bf16[2,128,512]{2,1,0:T(8,128)(2,1)S(1)}, bf16[2,128,512]{2,1,0:T(8,128)(2,1)}, u32[]{:S(2)}, u32[]{:S(2)}) collective-permute-start(bf16[2,128,512]{2,1,0:T(8,128)(2,1)S(1)} %pad_maximum_fusion.3), channel_id=1, source_target_pairs={{8,0},{16,8},{24,16},{32,24},{40,32},{48,40},{56,48},{64,56},{72,6... | collective-permute-start | bytes 786440 | tf_op jit(solution)/shard_map/ppermute | solution.py:40
  8.2 14.4 %collective-permute-start = (bf16[1,128,592]{2,1,0:T(8,128)(2,1)}, bf16[1,128,592]{2,1,0:T(8,128)(2,1)S(1)}, u32[]{:S(2)}, u32[]{:S(2)}) collective-permute-start(bf16[1,128,592]{2,1,0:T(8,128)(2,1)} %get-tuple-element.40), channel_id=1, source_target_pairs={{0,8},{8,16},{16,24},{24,32},{32,40},{40,48},{48,56},{56,64},{64,7... | collective-permute-start | bytes 454664 | tf_op jit(solution)/shard_map/ppermute | solution.py:39
  12.2 10.4 %collective-permute-start.1 = (bf16[1,128,592]{2,1,0:T(8,128)(2,1)S(1)}, bf16[1,128,592]{2,1,0:T(8,128)(2,1)S(1)}, u32[]{:S(2)}, u32[]{:S(2)}) collective-permute-start(bf16[1,128,592]{2,1,0:T(8,128)(2,1)S(1)} %get-tuple-element.41), channel_id=1, source_target_pairs={{8,0},{16,8},{24,16},{32,24},{40,32},{48,40},{56,48},{64,56},{72,6... | collective-permute-start | bytes 454664 | tf_op jit(solution)/shard_map/ppermute | solution.py:40
  22.6 48.1 %copy-start.13 = (bf16[1,128,592]{2,1,0:T(8,128)(2,1)}, bf16[1,128,592]{2,1,0:T(8,128)(2,1)S(1)}, u32[]{:S(2)}) copy-start(bf16[1,128,592]{2,1,0:T(8,128)(2,1)S(1)} %collective-permute-done.1) | copy-start | bytes 454660
  32.6 31.7 %all-to-all-start.4 = ((bf16[32,2,5120]{2,1,0:T(2,128)(2,1)}), bf16[32,2,5120]{2,1,0:T(2,128)(2,1)S(1)}, u32[]{:S(2)}, u32[]{:S(2)}) async-start(bf16[32,2,5120]{2,1,0:T(2,128)(2,1)} %reshape.189), calls=%async_computation.4 | async-start | bytes 1310720 | tf_op jit(solution)/shard_map/all_to_all | solution.py:129
  53.2 16.1 %copy-start.21 = (bf16[1,2,128,80]{2,3,1,0:T(8,128)(2,1)S(1)}, bf16[1,2,128,80]{2,3,1,0:T(8,128)(2,1)}, u32[]{:S(2)}) copy-start(bf16[1,2,128,80]{2,3,1,0:T(8,128)(2,1)} %param.14) | copy-start | bytes 122884
  65.2 60.0 %all-to-all-start.2 = ((f32[32,8,2304]{2,1,0:T(8,128)}), f32[32,8,2304]{2,1,0:T(8,128)S(1)}, u32[]{:S(2)}, u32[]{:S(2)}) async-start(f32[32,8,2304]{2,1,0:T(8,128)} %fusion.21), calls=%async_computation.2 | async-start | bytes 4718592 | tf_op jit(solution)/shard_map/all_to_all | solution.py:18
  75.2 5.5 %copy-start.9 = (bf16[2,128,336]{2,1,0:T(8,128)(2,1)S(1)}, bf16[2,128,336]{2,1,0:T(8,128)(2,1)}, u32[]{:S(2)}) copy-start(bf16[2,128,336]{2,1,0:T(8,128)(2,1)} %get-tuple-element.38) | copy-start | bytes 516100
  80.6 5.3 %copy-start.10 = (bf16[256,336]{0,1:T(8,128)(2,1)S(1)}, bf16[256,336]{0,1:T(8,128)(2,1)}, u32[]{:S(2)}) copy-start(bf16[256,336]{0,1:T(8,128)(2,1)} %copy.98) | copy-start | bytes 516100
  81.1 7.0 %copy-start.17 = (bf16[256,256]{0,1:T(8,128)(2,1)S(1)}, bf16[256,256]{0,1:T(8,128)(2,1)}, u32[]{:S(2)}) copy-start(bf16[256,256]{0,1:T(8,128)(2,1)} %copy.123) | copy-start | bytes 393220
  81.1 10.4 %copy-start.14 = (bf16[2,128,256]{2,1,0:T(8,128)(2,1)S(1)}, bf16[2,128,256]{2,1,0:T(8,128)(2,1)}, u32[]{:S(2)}) copy-start(bf16[2,128,256]{2,1,0:T(8,128)(2,1)} %get-tuple-element.43) | copy-start | bytes 393220
  95.2 35.6 %copy-start.19 = (s32[118,128]{1,0:T(8,128)S(1)}, s32[118,128]{1,0:T(8,128)}, u32[]{:S(2)}) copy-start(s32[118,128]{1,0:T(8,128)} %param.21) | copy-start | bytes 181252
  126.7 76.9 %all-to-all-start = ((f32[32,8,3024]{2,1,0:T(8,128)}), f32[32,8,3024]{2,1,0:T(8,128)S(1)}, u32[]{:S(2)}, u32[]{:S(2)}) async-start(f32[32,8,3024]{2,1,0:T(8,128)} %fusion), calls=%async_computation | async-start | bytes 6291456 | tf_op jit(solution)/shard_map/all_to_all | solution.py:18
  131.4 84.6 %copy-start.23 = (bf16[1,80,128]{2,1,0:T(8,128)(2,1)S(1)}, bf16[1,80,128]{2,1,0:T(8,128)(2,1)}, u32[]{:S(2)}) copy-start(bf16[1,80,128]{2,1,0:T(8,128)(2,1)} %param.19) | copy-start | bytes 61444
  133.2 85.2 %copy-start.22 = (bf16[1,118,128]{2,1,0:T(8,128)(2,1)S(1)}, bf16[1,118,128]{2,1,0:T(8,128)(2,1)}, u32[]{:S(2)}) copy-start(bf16[1,118,128]{2,1,0:T(8,128)(2,1)} %param.18) | copy-start | bytes 90628
  133.2 85.8 %copy-start.12 = (bf16[2,128,336]{1,2,0:T(8,128)(2,1)S(1)}, bf16[2,128,336]{1,2,0:T(8,128)(2,1)}, u32[]{:S(2)}) copy-start(bf16[2,128,336]{1,2,0:T(8,128)(2,1)} %copy-done.11) | copy-start | bytes 516100
  203.6 21.2 %copy-start.1 = (f32[32,8,3024]{2,1,0:T(8,128)}, f32[32,8,3024]{2,1,0:T(8,128)S(1)}, u32[]{:S(2)}) copy-start(f32[32,8,3024]{2,1,0:T(8,128)S(1)} %all-to-all-done) | copy-start | bytes 9289732
  204.5 61.5 %all-to-all-start.3 = ((f32[8,8,2304]{2,1,0:T(8,128)}), f32[8,8,2304]{2,1,0:T(8,128)}, u32[]{:S(2)}, u32[]{:S(2)}) async-start(f32[8,8,2304]{2,1,0:T(8,128)} %broadcast_in_dim.62), calls=%async_computation.3 | async-start | bytes 1179648 | tf_op jit(solution)/shard_map/all_to_all | solution.py:24
  224.8 8.2 %copy-start.18 = (s32[15360]{0:T(1024)S(1)}, s32[15360]{0:T(1024)}, u32[]{:S(2)}) copy-start(s32[15360]{0:T(1024)} %pad_clamp_fusion) | copy-start | bytes 184324
  267.0 28.0 %all-to-all-start.1 = ((f32[8,8,3024]{2,1,0:T(8,128)}), f32[8,8,3024]{2,1,0:T(8,128)S(1)}, u32[]{:S(2)}, u32[]{:S(2)}) async-start(f32[8,8,3024]{2,1,0:T(8,128)} %broadcast_in_dim.61), calls=%async_computation.1 | async-start | bytes 1572864 | tf_op jit(solution)/shard_map/all_to_all | solution.py:24
  276.6 8.0 %copy-start = (bf16[15104,80]{1,0:T(8,128)(2,1)S(1)}, bf16[15104,80]{1,0:T(8,128)(2,1)}, u32[]{:S(2)}) copy-start(bf16[15104,80]{1,0:T(8,128)(2,1)} %gather_fusion.1) | copy-start | bytes 7249924
  276.6 8.0 %copy-start.20 = (f32[128,118]{0,1:T(8,128)S(1)}, f32[128,118]{0,1:T(8,128)}, u32[]{:S(2)}) copy-start(f32[128,118]{0,1:T(8,128)} %bitcast_convert_fusion) | copy-start | bytes 181252
  (12 other events, 16.1 us)
where the time goes:
time: 300 us; the launch traced here: 296 us
  waiting for transfers between devices  114 us (38%)
  local copies, waits for them, and re-layouts  85.9 us (29%)
  starting transfers between devices  50.6 us (17%)
  other arithmetic  35.3 us (12%)
  matrix products  8.41 us (3%)
    all_to_all x2, waiting for transfers between devices, sent_and_summed(): blocks = lax.all_to_all(split_up(x, dim, devices), axis, 0, 0, tiled=True)  100 us
    gather x1, local copies, waits for them, and re-layouts, shards(): gathered = jnp.take(received_rows, point_slot, axis=0)  31 us
    unnamed x93, local copies, waits for them, and re-layouts  29.8 us
    all_to_all x2, starting transfers between devices, sent_to_all(): return lax.all_to_all(copies, axis, split_axis=0, concat_axis=0, tiled=True)  21.1 us
    all_to_all x1, starting transfers between devices, shards(): lax.all_to_all(outgoing, 'space', split_axis=0, concat_axis=0, tiled=True)  12.3 us
    all_to_all x1, waiting for transfers between devices, shards(): lax.all_to_all(outgoing, 'space', split_axis=0, concat_axis=0, tiled=True)  11.2 us
    concatenate x13, local copies, waits for them, and re-layouts, taps_of(): return jnp.concatenate(pieces, axis=-1).reshape(out_rows * out_cols, -1)  10.4 us
    all_to_all x2, starting transfers between devices, sent_and_summed(): blocks = lax.all_to_all(split_up(x, dim, devices), axis, 0, 0, tiled=True)  8.12 us
  transfers between devices with their start and end apart: 9, of which 4 were waited for; matrix products, arithmetic and copies ran while one was open for 38% of the time, Pallas kernels for 0%

commit v1 on v0

v1 whole, which is shorter than its diff:
```python
import functools
import math

import jax
import jax.numpy as jnp
from jax import lax
from jax.experimental import pallas as pl
from jax.experimental.pallas import tpu as pltpu
from jax.sharding import PartitionSpec as P

f32 = jnp.float32
bf16 = jnp.bfloat16
NN = (((1,), (0,)), ((), ()))
NT = (((1,), (1,)), ((), ()))
TN = (((0,), (0,)), ((), ()))


def mm(a, b, dims):
    return lax.dot_general(a, b, dims, preferred_element_type=f32)


def shifted_columns(rows, step, cols):
    if step == 0:
        return rows
    zero = jnp.zeros((1, rows.shape[1]), rows.dtype)
    out = []
    for r in range(rows.shape[0] // cols):
        row = rows[r * cols : (r + 1) * cols]
        out += [row[1:], zero] if step > 0 else [zero, row[:-1]]
    return jnp.concatenate(out, axis=0)

TILE = 128


def local_kernel(dims, own_ref, first_ref, before_ref, after_ref, lid_ref, cam_ref, wa_ref, wb_ref, list_ref, core_ref,
                 lidar_ref, blocks_ref, keep_ref, send_ref, g_ref, a_ref, gt_ref, at_ref):
    cols, ch, cam, parts = dims
    lid = lid_ref.shape[2]
    fan = cam + lid
    half = ch // 2
    ext = jnp.concatenate(
        [before_ref[0], before_ref[1], own_ref[0], own_ref[1], after_ref[0], after_ref[1]], axis=0
    ).astype(f32)
    for b in range(3):
        moved = shifted_columns(ext, b - 1, cols)
        g_ref[b] = moved.astype(bf16)
        gt_ref[b] = moved[cols : 5 * cols].T.astype(bf16)
    back = jnp.zeros((4 * cols, ch), f32)
    for a in range(3):
        for b in range(3):
            tap = (3 * (2 - a) + (2 - b)) * ch
            back += mm(g_ref[b, a * cols : (a + 4) * cols, :], wb_ref[:, tap : tap + ch], NN)
    first = jnp.concatenate([before_ref[2], first_ref[0], first_ref[1], after_ref[2]], axis=0).astype(f32)
    grad_a = jnp.where(first > 0, back, 0.0).astype(bf16).astype(f32)
    for b in range(3):
        moved = shifted_columns(grad_a, b - 1, cols)
        a_ref[b] = moved.astype(bf16)
        at_ref[b] = moved.T.astype(bf16)
    lidar = jnp.zeros((2 * cols, lid), f32)
    camera = jnp.zeros((cam, 2 * cols), f32)
    for a in range(3):
        for b in range(3):
            tap = (3 * (2 - a) + (2 - b)) * fan
            rows = a_ref[b, a * cols : (a + 2) * cols, :]
            lidar += mm(rows, wa_ref[tap + cam : tap + fan, :], NT)
            camera += mm(wa_ref[tap : tap + cam, :], rows, NT)
    for r in range(2):
        lidar_ref[r] = lidar[r * cols : (r + 1) * cols].astype(bf16)
    low = camera[:, :cols].astype(bf16)
    high = camera[:, cols:].astype(bf16)
    for k in range(blocks_ref.shape[0]):
        @pl.when(list_ref[k] > 0)
        def _():
            blocks_ref[k] = high

        @pl.when(list_ref[k] <= 0)
        def _():
            blocks_ref[k] = low

    second_core = core_ref[0] > 0
    per_part = keep_ref.shape[2] // TILE

    def put(value, tile):
        halves = value.reshape(ch // 16, 2, 8, value.shape[1])
        even = halves[:, 0].reshape(half, value.shape[1])
        odd = halves[:, 1].reshape(half, value.shape[1])
        mine = jnp.where(second_core, odd, even)
        other = jnp.where(second_core, even, odd).astype(bf16)
        for t in range(value.shape[1] // TILE):
            part, at = divmod(tile + t, per_part)
            here = slice(at * TILE, (at + 1) * TILE)
            keep_ref[part, :, here] = mine[:, t * TILE : (t + 1) * TILE]
            send_ref[part, :, here] = other[:, t * TILE : (t + 1) * TILE]

    hidden = jnp.maximum(jnp.concatenate([first_ref[0], first_ref[1]], axis=0), 0)
    lidar_in = jnp.concatenate([lid_ref[0], lid_ref[1]], axis=0)
    camera_in = jnp.concatenate([cam_ref[0], cam_ref[1]], axis=1)
    b_tiles, a_tiles = ch // TILE, lid // TILE
    packed = []
    for a in range(3):
        for b in range(3):
            tap = 3 * a + b
            window = slice((2 - a) * cols, (4 - a) * cols)
            put(mm(gt_ref[2 - b, :, window], hidden, NN), tap * b_tiles)
            put(mm(at_ref[2 - b, :, window], lidar_in, NN), 9 * b_tiles + tap * a_tiles)
            packed.append(mm(at_ref[2 - b, :, window], camera_in, NT))
    at = 9 * (b_tiles + a_tiles)
    spare = (parts * per_part - at) * TILE - 9 * cam
    packed.append(jnp.zeros((ch, spare), f32))
    put(jnp.concatenate(packed, axis=1), at)


def depth_kernel(blocks_ref, weight_ref, context_ref, slot_ref, gc_ref, gd_ref, wt_ref, st_ref, s_ref, m_ref, d_ref):
    sources, cam, cells_of = blocks_ref.shape
    depth, pix = slot_ref.shape
    wide = st_ref.shape[1]
    wt_ref[...] = jnp.concatenate([weight_ref[...].astype(f32), jnp.zeros((wide - depth, pix), f32)], axis=0).T
    st_ref[...] = jnp.concatenate([slot_ref[...], jnp.full((wide - depth, pix), -1, jnp.int32)], axis=0).T
    context_t = context_ref[...].astype(f32).T.astype(bf16)
    for s in range(sources):
        s_ref[:, s, :] = mm(context_t, blocks_ref[s], NN)
    cells = lax.broadcasted_iota(jnp.int32, (cells_of, wide), 0)
    places = lax.broadcasted_iota(jnp.int32, (sources, wide), 0)
    shift = cells_of.bit_length() - 1

    def pixels(g, carry):
        base = pl.multiple_of(g * 8, 8)
        slots = st_ref[pl.ds(base, 8), :]
        weights = wt_ref[pl.ds(base, 8), :]
        found_rows = []
        for k in range(8):
            slot = slots[k : k + 1]
            at_cell = jnp.where(cells == (slot & (cells_of - 1)), 1.0, 0.0).astype(bf16)
            here = places == (slot >> shift)
            m_ref[base + k] = mm(jnp.where(here, weights[k : k + 1], 0.0).astype(bf16), at_cell, NT)
            value = s_ref[base + k]
            top = value.astype(bf16)
            rest = (value - top.astype(f32)).astype(bf16)
            found = mm(jnp.concatenate([top, rest], axis=0), at_cell, NN)
            found = found[:sources] + found[sources:]
            found_rows.append(jnp.sum(jnp.where(here, found, 0.0), axis=0, keepdims=True))
        d_ref[pl.ds(base, 8), :] = jnp.concatenate(found_rows, axis=0)
        return carry

    lax.fori_loop(0, pix // 8, pixels, 0)
    gd_ref[...] = d_ref[...].T[:depth]
    total = jnp.zeros((cam, pix), f32)
    for s in range(sources):
        mass = m_ref[:, s, :]
        top = mass.astype(bf16)
        rest = (mass - top.astype(f32)).astype(bf16)
        total += mm(blocks_ref[s], top, NT) + mm(blocks_ref[s], rest, NT)
    gc_ref[...] = total


def call(kernel, outs, scratch, args, specs, flops, traffic, limit=40):
    return pl.pallas_call(
        kernel,
        out_shape=outs,
        in_specs=specs,
        out_specs=[VM] * len(outs),
        scratch_shapes=scratch,
        cost_estimate=pl.CostEstimate(flops=flops, bytes_accessed=traffic, transcendentals=0),
        compiler_params=pltpu.CompilerParams(vmem_limit_bytes=limit << 20),
    )(*args)


VM = pl.BlockSpec(memory_space=pltpu.VMEM)
SM = pl.BlockSpec(memory_space=pltpu.SMEM)


def neighbours(x, reverse):
    n = lax.axis_size("space")
    pairs = [(i, i + 1) for i in range(n - 1)]
    return lax.ppermute(x, "space", [(j, i) for i, j in pairs] if reverse else pairs)


def exchanged(x, axis, groups):
    return lax.all_to_all(x, axis, 0, 0, axis_index_groups=groups, tiled=True)


def summed(x):
    return jnp.sum(x.astype(f32), axis=0)


def shards(
    grad_out, pre_second, pre_first, camera_bev, lidar_bev, weight_a, weight_b,
    depth_weights, context, block_list, point_slot,
):
    _, rows, cols, ch = grad_out.shape
    cam, lid = camera_bev.shape[-1], lidar_bev.shape[-1]
    space, scenes = lax.axis_size("space"), lax.axis_size("scene")
    pix = point_slot.shape[1]
    place = space // 2
    reach = scenes // 2
    scale = 1.0 / math.sqrt(rows * cols * space * scenes)
    first = pre_first[0]
    grad_b = jnp.where(pre_second[0] > 0, grad_out[0], jnp.zeros((), bf16))
    before = neighbours(jnp.concatenate([grad_b, first[-1:]]), False)
    after = neighbours(jnp.concatenate([grad_b, first[:1]]), True)
    camera = jnp.swapaxes(camera_bev[0], 1, 2)
    listing = block_list[:, 0, 0]
    core = (lax.axis_index("space") % 2).reshape(1)

    tiles = 9 * (ch + lid) // TILE + -(-9 * cam // TILE)
    per_part = -(-tiles // reach) * TILE
    shape = jax.ShapeDtypeStruct
    lidar, blocks, keep, send = call(
        functools.partial(local_kernel, (cols, ch, cam, reach)),
        [
            shape((rows, cols, lid), bf16),
            shape((space, cam, cols), bf16),
            shape((reach, ch // 2, per_part), f32),
            shape((reach, ch // 2, per_part), bf16),
        ],
        [
            pltpu.VMEM((3, 6 * cols, ch), bf16),
            pltpu.VMEM((3, 4 * cols, ch), bf16),
            pltpu.VMEM((3, ch, 4 * cols), bf16),
            pltpu.VMEM((3, ch, 4 * cols), bf16),
        ],
        (grad_b, first, before, after, lidar_bev[0], camera, weight_a.T, weight_b, listing, core),
        [VM] * 8 + [SM] * 2,
        1_800_000_000,
        12_000_000,
    )
    incoming = exchanged(blocks, "space", None)
    other = lax.ppermute(send, "space", [(i, i ^ 1) for i in range(space)])
    pair = (keep + other.astype(f32)).astype(bf16)
    along_x = exchanged(pair, "scene", [[2 * i + h for i in range(reach)] for h in range(2)])
    part = summed(along_x).astype(bf16).reshape(place, 8, per_part)
    incoming, part = lax.optimization_barrier((incoming, part))
    along_yz = exchanged(part, "space", [[2 * i + c for i in range(place)] for c in range(2)])
    grad_context, grad_depth = call(
        depth_kernel,
        [shape((cam, pix), f32), shape(point_slot.shape, f32)],
        [
            pltpu.VMEM((pix, 128), f32),
            pltpu.VMEM((pix, 128), jnp.int32),
            pltpu.VMEM((pix, space, cols), f32),
            pltpu.VMEM((pix, space, cols), f32),
            pltpu.VMEM((pix, 128), f32),
        ],
        (incoming, depth_weights[0], context[0], point_slot),
        [VM] * 4,
        2_000_000_000,
        2_000_000,
    )
    own = summed(along_yz).astype(bf16)
    all_parts = exchanged(jnp.broadcast_to(own, (scenes, 8, per_part)), "scene", None)
    whole = summed(jnp.moveaxis(all_parts.reshape(reach, 2, 8, per_part), 1, 0))
    whole = jnp.moveaxis(whole, 0, 1).reshape(8, reach * per_part) * scale
    grad_wb = whole[:, : 9 * ch]
    lidar_part = whole[:, 9 * ch : 9 * (ch + lid)].reshape(8, 9, lid)
    camera_part = whole[:, 9 * (ch + lid) : 9 * (ch + lid + cam)].reshape(8, 9, cam)
    grad_wa = jnp.concatenate([camera_part, lidar_part], axis=2).reshape(8, 9 * (cam + lid))
    return grad_wa, grad_wb, lidar[None], grad_context[None], grad_depth[None]


def solution(mesh):
    field = P("scene", "space", None, None)
    pixels = P("scene", None, "space")
    return jax.shard_map(
        shards,
        mesh=mesh,
        in_specs=(field,) * 5 + (P(), P(), pixels, pixels, P(None, "space", None), P(None, "space")),
        out_specs=(P("space", None), P("space", None), field, pixels, pixels),
        check_vma=False,
    )
```

time: 300 us -> 122 us (0.41); the launches traced: 296 us -> 121 us
  waiting for transfers between devices: 114 us -> 23 us
  local copies, waits for them, and re-layouts: 85.9 us -> 9.69 us
  blocking collectives: 0 us -> 39.6 us
  other arithmetic: 35.3 us -> 1.84 us
  starting transfers between devices: 50.6 us -> 27.4 us
  Pallas kernels: 0 us -> 18.5 us
  matrix products: 8.41 us -> 0 us
    all_to_all x5 -> x2, waiting for transfers between devices: 114 us -> 19.1 us  [exchanged(): return lax.all_to_all(x, axis, 0, 0, axis_index_groups=groups, tiled=True)]
    all_to_all x0 -> x2, blocking collectives: none -> 39.6 us  [exchanged(): return lax.all_to_all(x, axis, 0, 0, axis_index_groups=groups, tiled=True)]
    gather x2 -> x0, local copies, waits for them, and re-layouts: 32 us -> none  [the longest x1 31 us: shards(): gathered = jnp.take(received_rows, point_slot, axis=0)]
    unnamed x93 -> x19, local copies, waits for them, and re-layouts: 29.8 us -> 6.61 us
    all_to_all x5 -> x2, starting transfers between devices: 41.5 us -> 20 us  [exchanged(): return lax.all_to_all(x, axis, 0, 0, axis_index_groups=groups, tiled=True)]
    pallas_call x0 -> x2, Pallas kernels: none -> 18.5 us  [call(): pl.pallas_call(kernel, out_shape=outs, in_specs=specs, out_specs=[VM] * l...]
    concatenate x13 -> x0, local copies, waits for them, and re-layouts: 10.4 us -> none  [taps_of(): return jnp.concatenate(pieces, axis=-1).reshape(out_rows * out_cols, -1)]
    dot_general x4 -> x0, matrix products: 8.41 us -> none  [the longest x2 6.83 us: reduce_weights(): jnp.dot(grad_flat.T, patches, preferred_element_type=jnp.float32)]
  transfers between devices with their start and end apart: 9 -> 5, of which waited for: 4 -> 3; matrix products, arithmetic and copies ran while one was open for 38% -> 1% of each run, Pallas kernels for 0% -> 11%
where the time goes in v1:
time: 122 us; the launch traced here: 121 us
  blocking collectives  39.6 us (32%)
  starting transfers between devices  27.4 us (22%)
  waiting for transfers between devices  23 us (19%)
  Pallas kernels  18.5 us (15%)
  local copies, waits for them, and re-layouts  9.69 us (8%)
  other arithmetic  1.84 us (2%)
    all_to_all x2, blocking collectives, exchanged(): return lax.all_to_all(x, axis, 0, 0, axis_index_groups=groups, tiled=True)  39.6 us
    all_to_all x2, starting transfers between devices, exchanged(): return lax.all_to_all(x, axis, 0, 0, axis_index_groups=groups, tiled=True)  20 us
    all_to_all x2, waiting for transfers between devices, exchanged(): return lax.all_to_all(x, axis, 0, 0, axis_index_groups=groups, tiled=True)  19.1 us
    pallas_call x2, Pallas kernels, call(): pl.pallas_call(kernel, out_shape=outs, in_specs=specs, out_specs=[VM] * l...  18.5 us
    unnamed x19, local copies, waits for them, and re-layouts  6.61 us
    ppermute x2, starting transfers between devices, neighbours(): lax.ppermute(x, 'space', [(j, i) for i, j in pairs] if reverse else pairs)  4.33 us
    ppermute x1, starting transfers between devices, shards(): other = lax.ppermute(send, 'space', [(i, i ^ 1) for i in range(space)])  3.08 us
    ppermute x1, waiting for transfers between devices, shards(): other = lax.ppermute(send, 'space', [(i, i ^ 1) for i in range(space)])  2.85 us
  transfers between devices with their start and end apart: 5, of which 3 were waited for; matrix products, arithmetic and copies ran while one was open for 1% of the time, Pallas kernels for 11%

profile of v1, /device:TPU:2, one launch (start us, length us, event | category | flops | bytes accessed | tf_op | source)
XLA Modules:
  0.0 120.9 jit_solution(1610560495445961384)
XLA Ops:
  0.6 0.9 slice_bitcast_fusion
  1.5 1.0 fusion.own_ref
  2.5 1.3 %collective-permute-start.1 = (bf16[3,128,256]{2,1,0:T(8,128)(2,1)S(1)}, bf16[3,128,256]{2,1,0:T(8,128)(2,1)S(1)}, u32[]{:S(2)}, u32[]{:S(2)}) collective-permute-start(bf16[3,128,256]{2,1,0:T(8,128)(2,1)S(1)} %get-tuple-element.38), channel_id=1, source_target_pairs={{8,0},{16,8},{24,16},{32,24},{40,32},{48,40},{56,48},{64,56},{72,6... | collective-permute-start | bytes 589832 | tf_op jit(solution)/shard_map/ppermute | solution.py:175
  3.8 3.0 %collective-permute-start = (bf16[3,128,256]{2,1,0:T(8,128)(2,1)S(1)}, bf16[3,128,256]{2,1,0:T(8,128)(2,1)S(1)}, u32[]{:S(2)}, u32[]{:S(2)}) collective-permute-start(bf16[3,128,256]{2,1,0:T(8,128)(2,1)S(1)} %get-tuple-element.39), channel_id=1, source_target_pairs={{0,8},{8,16},{16,24},{24,32},{32,40},{40,48},{48,56},{56,64},{64,7... | collective-permute-start | bytes 589832 | tf_op jit(solution)/shard_map/ppermute | solution.py:175
  6.9 1.0 collective-permute-done.before_ref
  7.9 0.9 copy-done
  8.8 1.4 %copy-done.1 = bf16[256,3024]{0,1:T(8,128)(2,1)S(1)} copy-done((bf16[256,3024]{0,1:T(8,128)(2,1)S(1)}, bf16[256,3024]{0,1:T(8,128)(2,1)}, u32[]{:S(2)}) %copy-start.1) | copy-done | bytes 1548312
  10.2 1.3 %copy-done.2 = bf16[256,2304]{1,0:T(8,128)(2,1)S(1)} copy-done((bf16[256,2304]{1,0:T(8,128)(2,1)S(1)}, bf16[256,2304]{1,0:T(8,128)(2,1)}, u32[]{:S(2)}) %copy-start.2) | copy-done | bytes 1179672
  11.5 0.9 copy-done.3
  12.4 0.8 copy-done.5
  13.2 0.7 copy-done.8
  13.9 5.1 %shard_map.146 = (bf16[2,128,256]{2,1,0:T(8,128)(2,1)}, bf16[32,80,128]{2,1,0:T(8,128)(2,1)}, f32[4,128,1408]{2,1,0:T(8,128)S(1)}, bf16[4,128,1408]{2,1,0:T(8,128)(2,1)S(1)}) custom-call(bf16[2,128,256]{2,1,0:T(8,128)(2,1)S(1)} %fusion.own_ref, bf16[2,128,256]{2,1,0:T(8,128)(2,1)S(1)} %bitcast.27, bf16[3,128,256]{2,1,0:T(8,128)(2,1)S(1)} %collective-permute-done.before_ref, ...), custom_call_target="tpu_custom_call" | custom-call | flops 1800000000 | bytes 12000000 | tf_op jit(solution)/shard_map/pallas_call | solution.py:157
  18.9 3.1 %collective-permute-start.2 = (bf16[4,128,1408]{2,1,0:T(8,128)(2,1)S(1)}, bf16[4,128,1408]{2,1,0:T(8,128)(2,1)S(1)}, u32[]{:S(2)}, u32[]{:S(2)}) collective-permute-start(bf16[4,128,1408]{2,1,0:T(8,128)(2,1)S(1)} %get-tuple-element.15), channel_id=1, source_target_pairs={{0,8},{8,0},{16,24},{24,16},{32,40},{40,32},{48,56},{56,48},{64,72... | collective-permute-start | bytes 4325384 | tf_op jit(solution)/shard_map/ppermute | solution.py:228
  22.0 2.8 %collective-permute-done.2 = bf16[4,128,1408]{2,1,0:T(8,128)(2,1)S(1)} collective-permute-done((bf16[4,128,1408]{2,1,0:T(8,128)(2,1)S(1)}, bf16[4,128,1408]{2,1,0:T(8,128)(2,1)S(1)}, u32[]{:S(2)}, u32[]{:S(2)}) %collective-permute-start.2) | collective-permute-done | bytes 1441824 | tf_op jit(solution)/shard_map/ppermute | solution.py:228
  25.2 23.0 %all_to_all.20 = bf16[4,128,1408]{2,1,0:T(8,128)(2,1)S(1)} all-to-all(bf16[4,128,1408]{2,1,0:T(8,128)(2,1)S(1)} %add_convert_fusion), channel_id=1, replica_groups={{0,2,4,6},{1,3,5,7},{8,10,12,14},{9,11,13,15},{16,18,20,22},{17,19,21,2..., dimensions={0} | all-to-all | bytes 2883584 | tf_op jit(solution)/shard_map/all_to_all | solution.py:179
  48.3 12.2 %all-to-all-start = ((bf16[32,80,128]{2,1,0:T(8,128)(2,1)}), bf16[32,80,128]{2,1,0:T(8,128)(2,1)S(1)}, u32[]{:S(2)}, u32[]{:S(2)}) async-start(bf16[32,80,128]{2,1,0:T(8,128)(2,1)} %get-tuple-element.13), calls=%async_computation | async-start | bytes 1310720 | tf_op jit(solution)/shard_map/all_to_all | solution.py:179
  60.7 19.1 %all-to-all-done.blocks_ref = bf16[32,80,128]{2,1,0:T(8,128)(2,1)S(1)} async-done(((bf16[32,80,128]{2,1,0:T(8,128)(2,1)}), bf16[32,80,128]{2,1,0:T(8,128)(2,1)S(1)}, u32[]{:S(2)}, u32[]{:S(2)}) %all-to-all-start) | async-done | bytes 655392 | tf_op jit(solution)/shard_map/all_to_all | solution.py:179
  79.9 16.6 %all_to_all.21 = bf16[16,8,1408]{2,1,0:T(8,128)(2,1)S(1)} all-to-all(bf16[16,8,1408]{2,1,0:T(8,128)(2,1)S(1)} %bitcast.35), channel_id=1, replica_groups={{0,16,32,48,64,80,96,112,128,144,160,176,192,208,224,240},{8,24,40,56,7..., dimensions={0} | all-to-all | bytes 720896 | tf_op jit(solution)/shard_map/all_to_all | solution.py:179
  96.5 0.7 broadcast_in_dim.14
  97.2 7.8 %all-to-all-start.3 = ((bf16[8,8,1408]{2,1,0:T(8,128)(2,1)}), bf16[8,8,1408]{2,1,0:T(8,128)(2,1)S(1)}, u32[]{:S(2)}, u32[]{:S(2)}) async-start(bf16[8,8,1408]{2,1,0:T(8,128)(2,1)} %broadcast_in_dim.14), calls=%async_computation.3 | async-start | bytes 360448 | tf_op jit(solution)/shard_map/all_to_all | solution.py:179
  105.1 13.4 %shard_map.147 = (f32[80,128]{1,0:T(8,128)}, f32[118,128]{1,0:T(8,128)S(1)}) custom-call(bf16[32,80,128]{2,1,0:T(8,128)(2,1)S(1)} %all-to-all-done.blocks_ref, bf16[118,128]{1,0:T(8,128)(2,1)S(1)} %bitcast.32, bf16[80,128]{1,0:T(8,128)(2,1)S(1)} %bitcast.33, s32[118,128]{1,0:T(8,128)S(1)} %copy-done.4), custom_call_target="tpu_custom_call" | custom-call | flops 2000000000 | bytes 2000000 | tf_op jit(solution)/shard_map/pallas_call | solution.py:157
  118.5 0.7 copy.22
  119.3 0.6 fusion.1
  120.2 0.7 reshape.41
  (24 shorter events, 1.0 us)
Async XLA Ops:
  2.5 4.4 %collective-permute-start.1 = (bf16[3,128,256]{2,1,0:T(8,128)(2,1)S(1)}, bf16[3,128,256]{2,1,0:T(8,128)(2,1)S(1)}, u32[]{:S(2)}, u32[]{:S(2)}) collective-permute-start(bf16[3,128,256]{2,1,0:T(8,128)(2,1)S(1)} %get-tuple-element.38), channel_id=1, source_target_pairs={{8,0},{16,8},{24,16},{32,24},{40,32},{48,40},{56,48},{64,56},{72,6... | collective-permute-start | bytes 589832 | tf_op jit(solution)/shard_map/ppermute | solution.py:175
  3.8 4.1 %collective-permute-start = (bf16[3,128,256]{2,1,0:T(8,128)(2,1)S(1)}, bf16[3,128,256]{2,1,0:T(8,128)(2,1)S(1)}, u32[]{:S(2)}, u32[]{:S(2)}) collective-permute-start(bf16[3,128,256]{2,1,0:T(8,128)(2,1)S(1)} %get-tuple-element.39), channel_id=1, source_target_pairs={{0,8},{8,16},{16,24},{24,32},{32,40},{40,48},{48,56},{56,64},{64,7... | collective-permute-start | bytes 589832 | tf_op jit(solution)/shard_map/ppermute | solution.py:175
  7.9 0.9 copy-start
  8.8 1.4 %copy-start.1 = (bf16[256,3024]{0,1:T(8,128)(2,1)S(1)}, bf16[256,3024]{0,1:T(8,128)(2,1)}, u32[]{:S(2)}) copy-start(bf16[256,3024]{0,1:T(8,128)(2,1)} %param.16) | copy-start | bytes 4644868
  10.2 1.3 %copy-start.2 = (bf16[256,2304]{1,0:T(8,128)(2,1)S(1)}, bf16[256,2304]{1,0:T(8,128)(2,1)}, u32[]{:S(2)}) copy-start(bf16[256,2304]{1,0:T(8,128)(2,1)} %wb_ref.1) | copy-start | bytes 3538948
  11.5 0.9 copy-start.3
  12.4 0.8 copy-start.5
  13.2 0.7 copy-start.8
  18.9 5.9 %collective-permute-start.2 = (bf16[4,128,1408]{2,1,0:T(8,128)(2,1)S(1)}, bf16[4,128,1408]{2,1,0:T(8,128)(2,1)S(1)}, u32[]{:S(2)}, u32[]{:S(2)}) collective-permute-start(bf16[4,128,1408]{2,1,0:T(8,128)(2,1)S(1)} %get-tuple-element.15), channel_id=1, source_target_pairs={{0,8},{8,0},{16,24},{24,16},{32,40},{40,32},{48,56},{56,48},{64,72... | collective-permute-start | bytes 4325384 | tf_op jit(solution)/shard_map/ppermute | solution.py:228
  48.3 31.6 %all-to-all-start = ((bf16[32,80,128]{2,1,0:T(8,128)(2,1)}), bf16[32,80,128]{2,1,0:T(8,128)(2,1)S(1)}, u32[]{:S(2)}, u32[]{:S(2)}) async-start(bf16[32,80,128]{2,1,0:T(8,128)(2,1)} %get-tuple-element.13), calls=%async_computation | async-start | bytes 1310720 | tf_op jit(solution)/shard_map/all_to_all | solution.py:179
  60.5 44.6 %copy-start.4 = (s32[118,128]{1,0:T(8,128)S(1)}, s32[118,128]{1,0:T(8,128)}, u32[]{:S(2)}) copy-start(s32[118,128]{1,0:T(8,128)} %slot_ref.1) | copy-start | bytes 181252
  60.5 44.6 %copy-start.6 = (bf16[1,118,128]{2,1,0:T(8,128)(2,1)S(1)}, bf16[1,118,128]{2,1,0:T(8,128)(2,1)}, u32[]{:S(2)}) copy-start(bf16[1,118,128]{2,1,0:T(8,128)(2,1)} %param.18) | copy-start | bytes 90628
  60.5 44.6 %copy-start.7 = (bf16[1,80,128]{2,1,0:T(8,128)(2,1)S(1)}, bf16[1,80,128]{2,1,0:T(8,128)(2,1)}, u32[]{:S(2)}) copy-start(bf16[1,80,128]{2,1,0:T(8,128)(2,1)} %param.19) | copy-start | bytes 61444
  97.2 22.0 %all-to-all-start.3 = ((bf16[8,8,1408]{2,1,0:T(8,128)(2,1)}), bf16[8,8,1408]{2,1,0:T(8,128)(2,1)S(1)}, u32[]{:S(2)}, u32[]{:S(2)}) async-start(bf16[8,8,1408]{2,1,0:T(8,128)(2,1)} %broadcast_in_dim.14), calls=%async_computation.3 | async-start | bytes 360448 | tf_op jit(solution)/shard_map/all_to_all | solution.py:179
